TPU v7x, 32 devices: a whole 2x2x4 slice. The times are simulated.
32 devices in a mesh: space: 2 (over x), energy: 16 (over z, y, core).
Axes of the slice: x: 2, y: 2, z: 4, core: 2. Of those that a mesh axis runs over, the one named last changes fastest.
Arguments:
- lesser_in: bfloat16 [16, 2, 2, 256, 256], P('energy', 'space'), may hold values from -6 to 6
- retarded: bfloat16 [16, 2, 2, 256, 256], P('energy', 'space'), may hold values from -0.25 to 0.25
- coupling: bfloat16 [2, 2, 256, 256], P('space'), may hold values from -0.25 to 0.25
- interaction: bfloat16 [2, 32, 65536], P('space', None, 'energy'), may hold values from -1.5 to 1.5
Outputs:
- self_energy: bfloat16 [16, 2, 2, 256, 256], P('energy', 'space')
All inputs are finite; a program needn't handle non-finite values.
Results may differ from a plain program's by a relative error of at most 0.029.
Values may be sent and summed in bfloat16 or wider, within the bound.
A program may use at most 128 MiB of HBM per device.

v0:
```python
import math
import jax
import jax.numpy as jnp
from jax import lax
from jax.sharding import PartitionSpec as P


def product(left_real, left_imag, right_real, right_imag):
    real_part = jnp.dot(left_real, right_real, preferred_element_type=jnp.float32) - jnp.dot(
        left_imag, right_imag, preferred_element_type=jnp.float32
    )
    imag_part = jnp.dot(left_real, right_imag, preferred_element_type=jnp.float32) + jnp.dot(
        left_imag, right_real, preferred_element_type=jnp.float32
    )
    return (real_part, imag_part)


def phase_table(row_count, column_count, length):
    row_index = jnp.arange(row_count, dtype=jnp.int32)[:, None]
    column_index = jnp.arange(column_count, dtype=jnp.int32)[None, :]
    residue = row_index * column_index % length
    return residue.astype(jnp.float32) * (2.0 * math.pi / length)


def finish(spectrum_real, spectrum_imag, weights, energy_count, length):
    forward_scale = energy_count ** (-0.5)
    inverse_scale = length ** (-0.5)
    spectrum_real = spectrum_real * forward_scale
    spectrum_imag = spectrum_imag * forward_scale
    weight_values = weights.astype(jnp.float32)
    squared_real = (
        (spectrum_real * spectrum_real - spectrum_imag * spectrum_imag) * weight_values
    ).astype(jnp.bfloat16)
    squared_imag = (2.0 * spectrum_real * spectrum_imag * weight_values).astype(jnp.bfloat16)
    inverse_phase = phase_table(energy_count, length, length)
    inverse_real = jnp.cos(inverse_phase).astype(jnp.bfloat16)
    inverse_imag = jnp.sin(inverse_phase).astype(jnp.bfloat16)
    out_real, out_imag = product(inverse_real, inverse_imag, squared_real, squared_imag)
    return jnp.stack([out_real * inverse_scale, out_imag * inverse_scale], axis=1).astype(
        jnp.bfloat16
    )


def batched(pattern, former, latter):
    return jnp.einsum(pattern, former, latter, preferred_element_type=jnp.float32)


def local(lesser_in, retarded, coupling, interaction):
    local_count = lesser_in.shape[0]
    block_order = coupling.shape[-1]
    groups = lax.axis_size("energy")
    sections = lax.axis_size("space")
    energy_count = local_count * groups
    length = 2 * energy_count
    entry_width = block_order * block_order // groups
    resolvent_real = retarded[:, 0, 0]
    resolvent_imag = retarded[:, 0, 1]
    lesser_real = lesser_in[:, 0, 0]
    lesser_imag = lesser_in[:, 0, 1]
    coupling_real = coupling[0, 0]
    coupling_imag = coupling[0, 1]
    map_real = (
        batched("eij,jk->eik", resolvent_real, coupling_real)
        - batched("eij,jk->eik", resolvent_imag, coupling_imag)
    ).astype(jnp.bfloat16)
    map_imag = (
        batched("eij,jk->eik", resolvent_real, coupling_imag)
        + batched("eij,jk->eik", resolvent_imag, coupling_real)
    ).astype(jnp.bfloat16)
    half_real = (
        batched("eij,ejk->eik", resolvent_real, lesser_real)
        - batched("eij,ejk->eik", resolvent_imag, lesser_imag)
    ).astype(jnp.bfloat16)
    half_imag = (
        batched("eij,ejk->eik", resolvent_real, lesser_imag)
        + batched("eij,ejk->eik", resolvent_imag, lesser_real)
    ).astype(jnp.bfloat16)
    source_real = batched("eij,ekj->eik", half_real, resolvent_real) + batched(
        "eij,ekj->eik", half_imag, resolvent_imag
    )
    source_imag = batched("eij,ekj->eik", half_imag, resolvent_real) - batched(
        "eij,ekj->eik", half_real, resolvent_imag
    )
    forward_phase = phase_table(length, energy_count, length)
    forward_real = jnp.cos(forward_phase).astype(jnp.bfloat16)
    forward_imag = (-jnp.sin(forward_phase)).astype(jnp.bfloat16)
    padded = (local_count + sections - 1) // sections * sections
    extra = padded - local_count
    maps_all = jnp.pad(
        jnp.stack([map_real, map_imag], axis=1), ((0, extra), (0, 0), (0, 0), (0, 0))
    )
    sources_all = jnp.pad(
        jnp.stack([source_real, source_imag], axis=1), ((0, extra), (0, 0), (0, 0), (0, 0))
    )
    maps_here, sources_here = (
        lax.all_to_all(
            maps_all[:, None].astype(jnp.float32), "space", split_axis=0, concat_axis=1, tiled=True
        ).astype(jnp.bfloat16),
        lax.all_to_all(sources_all[:, None], "space", split_axis=0, concat_axis=1, tiled=True),
    )
    per_device = maps_here.shape[0]

    def link(carried, inputs_pair):
        step_map, step_source = inputs_pair
        carry_real = (
            batched("eij,ejk->eik", step_map[:, 0], carried[:, 0])
            - batched("eij,ejk->eik", step_map[:, 1], carried[:, 1])
        ).astype(jnp.bfloat16)
        carry_imag = (
            batched("eij,ejk->eik", step_map[:, 0], carried[:, 1])
            + batched("eij,ejk->eik", step_map[:, 1], carried[:, 0])
        ).astype(jnp.bfloat16)
        grown_real = batched("eij,ekj->eik", carry_real, step_map[:, 0]) + batched(
            "eij,ekj->eik", carry_imag, step_map[:, 1]
        )
        grown_imag = batched("eij,ekj->eik", carry_imag, step_map[:, 0]) - batched(
            "eij,ekj->eik", carry_real, step_map[:, 1]
        )
        fresh = jnp.stack(
            [step_source[:, 0] + grown_real, step_source[:, 1] + grown_imag], axis=1
        ).astype(jnp.bfloat16)
        return (fresh, fresh)

    start_block = jnp.zeros((per_device, 2, block_order, block_order), jnp.bfloat16)
    last_block, layers = lax.scan(
        link, start_block, (jnp.moveaxis(maps_here, 1, 0), jnp.moveaxis(sources_here, 1, 0))
    )
    greens = jnp.moveaxis(layers, 0, 1).reshape(per_device, sections, 2, block_order * block_order)
    homed = lax.all_to_all(
        lax.all_to_all(greens, "space", split_axis=1, concat_axis=0, tiled=True),
        "energy",
        split_axis=3,
        concat_axis=0,
        tiled=True,
    )
    entries = homed.reshape(groups, padded, 2, entry_width)[:, :local_count].reshape(
        energy_count, 2, entry_width
    )
    spectrum_real, spectrum_imag = product(forward_real, forward_imag, entries[:, 0], entries[:, 1])
    result = finish(spectrum_real, spectrum_imag, interaction[0], energy_count, length)
    returned = lax.all_to_all(result, "energy", split_axis=0, concat_axis=2, tiled=True)
    return returned.reshape(local_count, 1, 2, block_order, block_order)


def solution(mesh):
    in_specs = (
        P("energy", "space", None, None, None),
        P("energy", "space", None, None, None),
        P("space", None, None, None),
        P("space", None, "energy"),
    )
    out_specs = P("energy", "space", None, None, None)
    return jax.shard_map(local, mesh=mesh, in_specs=in_specs, out_specs=out_specs, check_vma=False)
```

profile of v0, /device:TPU:0, one launch (start us, length us, event | category | flops | bytes accessed | tf_op | source)
XLA Modules:
  0.0 321.3 jit_solution(13402352093027269052)
XLA Ops:
  0.0 1.1 fusion.41
  1.2 1.2 fusion.45
  2.3 1.2 fusion.31
  3.5 1.2 fusion.32
  5.5 4.2 %all-to-all-start.1 = ((bf16[2,1,2,256,256]{4,3,2,1,0:T(8,128)(2,1)}), bf16[2,1,2,256,256]{4,3,2,1,0:T(8,128)(2,1)S(1)}, u32[]{:S(2)}, u32[]{:S(2)}) async-start(bf16[2,1,2,256,256]{4,3,2,1,0:T(8,128)(2,1)} %fusion.40), calls=%async_computation.1 | async-start | bytes 1048576 | tf_op jit(solution)/shard_map/all_to_all | solution.py:96
  9.7 1.1 fusion.47
  10.9 1.2 fusion.57
  12.0 1.2 fusion.28
  13.2 1.1 fusion.61
  14.3 1.2 fusion.27
  15.5 1.1 fusion.64
  16.6 1.1 fusion.25
  17.7 1.1 fusion.26
  18.9 1.0 fusion.33
  19.9 3.6 %all-to-all-start = ((f32[2,1,2,256,256]{4,3,2,1,0:T(8,128)}), f32[2,1,2,256,256]{4,3,2,1,0:T(8,128)S(1)}, u32[]{:S(2)}, u32[]{:S(2)}) async-start(f32[2,1,2,256,256]{4,3,2,1,0:T(8,128)} %fusion.33), calls=%async_computation | async-start | bytes 2097152 | tf_op jit(solution)/shard_map/all_to_all | solution.py:99
  23.5 14.3 %all-to-all-done = f32[2,1,2,256,256]{4,3,2,1,0:T(8,128)S(1)} async-done(((f32[2,1,2,256,256]{4,3,2,1,0:T(8,128)}), f32[2,1,2,256,256]{4,3,2,1,0:T(8,128)S(1)}, u32[]{:S(2)}, u32[]{:S(2)}) %all-to-all-start) | async-done | bytes 1048608 | tf_op jit(solution)/shard_map/all_to_all | solution.py:99
  37.9 3.7 %while.12 = (s32[]{:T(128)}, bf16[1,2,256,256]{3,2,1,0:T(8,128)(2,1)S(1)}, bf16[2,1,2,256,256]{4,3,2,1,0:T(8,128)(2,1)S(1)}, f32[2,1,2,256,256]{4,3,2,1,0:T(8,12...) while((s32[]{:T(128)}, bf16[1,2,256,256]{3,2,1,0:T(8,128)(2,1)S(1)}, ...), condition=%wide.region_1.2_spmd, body=%wide.region_0.1_spmd.sunk | while | flops 269746176 | bytes 7864409 | solution.py:125
  41.7 10.1 %all_to_all.60 = bf16[1,2,2,65536]{3,2,0,1:T(2,128)(2,1)S(1)} all-to-all(bf16[1,2,2,65536]{3,2,0,1:T(2,128)(2,1)S(1)} %reshape_transpose.3), channel_id=1, replica_groups=mesh['space'=2,'energy'=16] {'space'}, dimensions={1} | all-to-all | bytes 1048576 | tf_op jit(solution)/shard_map/all_to_all | solution.py:130
  51.8 50.9 %copy.13 = bf16[2,1,2,65536]{2,0,1,3:T(2,128)(2,1)} copy(bf16[2,1,2,65536]{3,2,0,1:T(2,128)(2,1)S(1)} %bitcast.204) | data formatting | bytes 1048576 | tf_op jit(solution)/shard_map/all_to_all | solution.py:130
  102.7 61.2 %reshape.243 = bf16[16,2,8192]{2,1,0:T(2,128)(2,1)S(1)} reshape(bf16[65536,1,2,2]{3,2,1,0:T(2,128)(2,1)} %bitcast.198) | data formatting | bytes 1048576
  163.9 20.0 %all_to_all.61 = bf16[16,2,8192]{2,1,0:T(2,128)(2,1)S(1)} all-to-all(bf16[16,2,8192]{2,1,0:T(2,128)(2,1)S(1)} %reshape.243), channel_id=1, replica_groups=mesh['space'=2,'energy'=16] {'energy'}, dimensions={0} | all-to-all | bytes 1048576 | tf_op jit(solution)/shard_map/all_to_all | solution.py:129
  183.8 73.4 %reshape.244 = bf16[65536,1,2,2]{3,2,1,0:T(2,128)(2,1)} reshape(bf16[16,2,8192]{2,1,0:T(2,128)(2,1)S(1)} %all_to_all.61) | data formatting | bytes 1048576
  257.2 46.6 %copy.17 = bf16[2,1,2,16,4096]{4,3,2,0,1:T(8,128)(2,1)S(1)} copy(bf16[2,1,2,16,4096]{2,0,4,3,1:T(2,128)(2,1)} %bitcast.199) | data formatting | bytes 1048576 | tf_op jit(solution)/shard_map/all_to_all | solution.py:129
  306.3 14.0 %all_to_all.62 = bf16[16,2,4096]{2,1,0:T(2,128)(2,1)S(1)} all-to-all(bf16[16,2,4096]{2,1,0:T(2,128)(2,1)S(1)} %copy.15), channel_id=1, replica_groups=mesh['space'=2,'energy'=16] {'energy'}, dimensions={0} | all-to-all | bytes 524288 | tf_op jit(solution)/shard_map/all_to_all | solution.py:141
  (44 shorter events, 7.9 us)
Async XLA Ops:
  5.5 14.4 %all-to-all-start.1 = ((bf16[2,1,2,256,256]{4,3,2,1,0:T(8,128)(2,1)}), bf16[2,1,2,256,256]{4,3,2,1,0:T(8,128)(2,1)S(1)}, u32[]{:S(2)}, u32[]{:S(2)}) async-start(bf16[2,1,2,256,256]{4,3,2,1,0:T(8,128)(2,1)} %fusion.40), calls=%async_computation.1 | async-start | bytes 1048576 | tf_op jit(solution)/shard_map/all_to_all | solution.py:96
  19.9 17.9 %all-to-all-start = ((f32[2,1,2,256,256]{4,3,2,1,0:T(8,128)}), f32[2,1,2,256,256]{4,3,2,1,0:T(8,128)S(1)}, u32[]{:S(2)}, u32[]{:S(2)}) async-start(f32[2,1,2,256,256]{4,3,2,1,0:T(8,128)} %fusion.33), calls=%async_computation | async-start | bytes 2097152 | tf_op jit(solution)/shard_map/all_to_all | solution.py:99
  183.8 120.8 %copy-start = (bf16[1,32,4096]{2,1,0:T(8,128)(2,1)S(1)}, bf16[1,32,4096]{2,1,0:T(8,128)(2,1)}, u32[]{:S(2)}) copy-start(bf16[1,32,4096]{2,1,0:T(8,128)(2,1)} %param.9) | copy-start | bytes 786436
where the time goes:
time: 323 us; the launch traced here: 321 us
  local copies, waits for them, and re-layouts  234 us (72%)
  blocking collectives  44 us (14%)
  matrix products  19.1 us (6%)
  waiting for transfers between devices  14.3 us (4%)
  starting transfers between devices  7.81 us (2%)
    unnamed x4, local copies, waits for them, and re-layouts  135 us
    all_to_all x1, local copies, waits for them, and re-layouts, local(): lax.all_to_all(greens, 'space', split_axis=1, concat_axis=0, tiled=True)  50.9 us
    all_to_all x1, local copies, waits for them, and re-layouts, local(): lax.all_to_all(lax.all_to_all(greens, 'space', split_axis=1, concat_axis=...  46.6 us
    all_to_all x1, blocking collectives, local(): lax.all_to_all(lax.all_to_all(greens, 'space', split_axis=1, concat_axis=...  20 us
    dot_general x28, matrix products, batched(): jnp.einsum(pattern, former, latter, preferred_element_type=jnp.float32)  17 us
    all_to_all x1, waiting for transfers between devices, local(): lax.all_to_all(sources_all[:, None], 'space', split_axis=0, concat_axis=1...  14.3 us
    all_to_all x1, blocking collectives, local(): lax.all_to_all(result, 'energy', split_axis=0, concat_axis=2, tiled=True)  14 us
    all_to_all x1, blocking collectives, local(): lax.all_to_all(greens, 'space', split_axis=1, concat_axis=0, tiled=True)  10.1 us
  transfers between devices with their start and end apart: 2, of which 1 were waited for; matrix products, arithmetic and copies ran while one was open for 3% of the time, Pallas kernels for 0%

commit v1 on v0

--- a/solution.py
+++ b/solution.py
@@ -1,8 +1,22 @@
+import functools
 import math
 import jax
 import jax.numpy as jnp
 from jax import lax
 from jax.sharding import PartitionSpec as P
+
+
+def part_rings(body, comm_axis):
+    carry = jnp.concatenate(
+        jax.lax.all_to_all(
+            jnp.stack(jnp.split(body, jax.lax.psum(1, comm_axis), 3), 0), comm_axis, 0, 0
+        ),
+        0,
+    )
+    return carry
+
+
+refer_plane_over_axis = functools.partial(part_rings, comm_axis="energy")
 
 
 def product(left_real, left_imag, right_real, right_imag):
@@ -126,12 +140,8 @@
         link, start_block, (jnp.moveaxis(maps_here, 1, 0), jnp.moveaxis(sources_here, 1, 0))
     )
     greens = jnp.moveaxis(layers, 0, 1).reshape(per_device, sections, 2, block_order * block_order)
-    homed = lax.all_to_all(
-        lax.all_to_all(greens, "space", split_axis=1, concat_axis=0, tiled=True),
-        "energy",
-        split_axis=3,
-        concat_axis=0,
-        tiled=True,
+    homed = refer_plane_over_axis(
+        lax.all_to_all(greens, "space", split_axis=1, concat_axis=0, tiled=True)
     )
     entries = homed.reshape(groups, padded, 2, entry_width)[:, :local_count].reshape(
         energy_count, 2, entry_width

time: 323 us -> 85.6 us (0.27)
  local copies, waits for them, and re-layouts: 234 us -> 3.51 us
  matrix products: 19.1 us -> 8.97 us
  waiting for transfers between devices: 14.3 us -> 19.3 us
    unnamed x4 -> x23, local copies, waits for them, and re-layouts: 135 us -> 1.14 us
    all_to_all x2 -> x0, local copies, waits for them, and re-layouts: 97.4 us -> none  [the longest x1 50.9 us: local(): lax.all_to_all(greens, 'space', split_axis=1, concat_axis=0, tiled=True)]
    dot_general x28, matrix products: 17 us -> 6.64 us  [batched(): jnp.einsum(pattern, former, latter, preferred_element_type=jnp.float32)]
    all_to_all x1, waiting for transfers between devices: 0.01 us -> 6 us  [local(): lax.all_to_all(maps_all[:, None].astype(jnp.float32), 'space', split_axis...]
  transfers between devices with their start and end apart: 2 -> 2, of which waited for: 1 -> 2; matrix products, arithmetic and copies ran while one was open for 3% -> 3% of each run, Pallas kernels for 0% -> 0%
where the time goes in v1:
time: 85.6 us; the launch traced here: 85.1 us
  blocking collectives  43 us (50%)
  waiting for transfers between devices  19.3 us (23%)
  matrix products  8.97 us (10%)
  starting transfers between devices  7.94 us (9%)
  local copies, waits for them, and re-layouts  3.51 us (4%)
  other arithmetic  2.05 us (2%)
    all_to_all x1, blocking collectives, part_rings(): jax.lax.all_to_all(jnp.stack(jnp.split(body, jax.lax.psum(1, comm_axis),...  19.7 us
    all_to_all x1, blocking collectives, local(): lax.all_to_all(result, 'energy', split_axis=0, concat_axis=2, tiled=True)  14 us
    all_to_all x1, waiting for transfers between devices, local(): lax.all_to_all(sources_all[:, None], 'space', split_axis=0, concat_axis=1...  13.3 us
    all_to_all x1, blocking collectives, local(): lax.all_to_all(greens, 'space', split_axis=1, concat_axis=0, tiled=True)  9.24 us
    dot_general x28, matrix products, batched(): jnp.einsum(pattern, former, latter, preferred_element_type=jnp.float32)  6.64 us
    all_to_all x1, waiting for transfers between devices, local(): lax.all_to_all(maps_all[:, None].astype(jnp.float32), 'space', split_axis...  6 us
    all_to_all x1, starting transfers between devices, local(): lax.all_to_all(maps_all[:, None].astype(jnp.float32), 'space', split_axis...  4.36 us
    all_to_all x1, starting transfers between devices, local(): lax.all_to_all(sources_all[:, None], 'space', split_axis=0, concat_axis=1...  3.58 us
  transfers between devices with their start and end apart: 2, of which 2 were waited for; matrix products, arithmetic and copies ran while one was open for 3% of the time, Pallas kernels for 0%

profile of v1, /device:TPU:0, one launch (start us, length us, event | category | flops | bytes accessed | tf_op | source)
XLA Modules:
  0.0 85.1 jit_solution(2266567847947035270)
XLA Ops:
  0.0 1.2 %fusion.47 = f32[256,256]{1,0:T(8,128)S(1)} fusion(bf16[1,2,256,256]{3,2,1,0:T(8,128)(2,1)} %param.8, bf16[1,1,2,256,256]{4,3,2,1,0:T(8,128)(2,1)} %param.7), kind=kOutput, calls=%fused_computation.75 | convolution fusion | flops 33554432 | bytes 524288 | tf_op jit(solution)/shard_map/eij,jk->eik/dot_general | solution.py:59
  1.8 0.9 %fusion.40 = bf16[2,1,2,256,256]{4,3,2,1,0:T(8,128)(2,1)} fusion(bf16[1,1,256,256]{3,2,1,0:T(8,128)(2,1)S(1)} %fusion.31, bf16[1,1,256,256]{3,2,1,0:T(8,128)(2,1)S(1)} %fusion.32), kind=kLoop, calls=%fused_computation.66 | loop fusion | flops 1835008 | bytes 786432 | tf_op jit(solution)/shard_map/convert_element_type | solution.py:111
  2.7 4.4 %all-to-all-start.1 = ((bf16[2,1,2,256,256]{4,3,2,1,0:T(8,128)(2,1)}), bf16[2,1,2,256,256]{4,3,2,1,0:T(8,128)(2,1)S(1)}, u32[]{:S(2)}, u32[]{:S(2)}) async-start(bf16[2,1,2,256,256]{4,3,2,1,0:T(8,128)(2,1)} %fusion.40), calls=%async_computation.1 | async-start | bytes 1048576 | tf_op jit(solution)/shard_map/all_to_all | solution.py:110
  8.3 0.2 fusion.25
  8.5 0.2 fusion.26
  8.7 1.0 %fusion.33 = f32[2,1,2,256,256]{4,3,2,1,0:T(8,128)} fusion(f32[1,1,256,256]{3,2,1,0:T(8,128)S(1)} %fusion.25, f32[1,1,256,256]{3,2,1,0:T(8,128)S(1)} %fusion.26), kind=kLoop, calls=%fused_computation.56 | loop fusion | flops 1048576 | bytes 1572864 | tf_op jit(solution)/shard_map/broadcast_in_dim | solution.py:113
  9.8 6.0 %all-to-all-done.1 = bf16[2,1,2,256,256]{4,3,2,1,0:T(8,128)(2,1)S(1)} async-done(((bf16[2,1,2,256,256]{4,3,2,1,0:T(8,128)(2,1)}), bf16[2,1,2,256,256]{4,3,2,1,0:T(8,128)(2,1)S(1)}, u32[]{:S(2)}, u32[]{:S(2)}) %all-to-all-start.1) | async-done | bytes 524320 | tf_op jit(solution)/shard_map/all_to_all | solution.py:110
  15.8 3.6 %all-to-all-start = ((f32[2,1,2,256,256]{4,3,2,1,0:T(8,128)}), f32[2,1,2,256,256]{4,3,2,1,0:T(8,128)S(1)}, u32[]{:S(2)}, u32[]{:S(2)}) async-start(f32[2,1,2,256,256]{4,3,2,1,0:T(8,128)} %fusion.33), calls=%async_computation | async-start | bytes 2097152 | tf_op jit(solution)/shard_map/all_to_all | solution.py:113
  19.4 13.3 %all-to-all-done = f32[2,1,2,256,256]{4,3,2,1,0:T(8,128)S(1)} async-done(((f32[2,1,2,256,256]{4,3,2,1,0:T(8,128)}), f32[2,1,2,256,256]{4,3,2,1,0:T(8,128)S(1)}, u32[]{:S(2)}, u32[]{:S(2)}) %all-to-all-start) | async-done | bytes 1048608 | tf_op jit(solution)/shard_map/all_to_all | solution.py:113
  32.7 3.7 %while.12 = (s32[]{:T(128)}, bf16[1,2,256,256]{3,2,1,0:T(8,128)(2,1)S(1)}, bf16[2,1,2,256,256]{4,3,2,1,0:T(8,128)(2,1)S(1)}, f32[2,1,2,256,256]{4,3,2,1,0:T(8,12...) while((s32[]{:T(128)}, bf16[1,2,256,256]{3,2,1,0:T(8,128)(2,1)S(1)}, ...), condition=%wide.region_1.2_spmd, body=%wide.region_0.1_spmd.sunk | while | flops 269746176 | bytes 7864401 | solution.py:139
  33.8 0.2 fusion.187
  35.6 0.2 fusion.187
  36.1 0.2 fusion.185
  36.6 9.2 %all_to_all.50 = bf16[1,2,2,65536]{3,2,0,1:T(2,128)(2,1)S(1)} all-to-all(bf16[1,2,2,65536]{3,2,0,1:T(2,128)(2,1)S(1)} %reshape_transpose.3), channel_id=1, replica_groups=mesh['space'=2,'energy'=16] {'space'}, dimensions={1} | all-to-all | bytes 1048576 | tf_op jit(solution)/shard_map/all_to_all | solution.py:144
  46.4 19.7 %all_to_all.51 = bf16[16,2,1,2,4096]{4,3,1,2,0:T(2,128)(2,1)S(1)} all-to-all(bf16[16,2,1,2,4096]{4,3,1,2,0:T(2,128)(2,1)S(1)} %constant_dynamic-update-slice_fusion), channel_id=1, replica_groups=mesh['space'=2,'energy'=16] {'energy'}, dimensions={0} | all-to-all | bytes 1048576 | tf_op jit(solution)/shard_map/all_to_all | solution.py:11
  66.3 0.6 fusion.143
  66.9 0.3 fusion.45
  67.2 0.3 fusion.41
  67.6 0.3 convolution_subtract_fusion.2
  67.9 0.6 copy-done.3
  68.5 0.4 fusion.36
  69.9 0.3 copy.31
  70.2 14.0 %all_to_all.52 = bf16[16,2,4096]{2,1,0:T(2,128)(2,1)S(1)} all-to-all(bf16[16,2,4096]{2,1,0:T(2,128)(2,1)S(1)} %copy.31), channel_id=1, replica_groups=mesh['space'=2,'energy'=16] {'energy'}, dimensions={0} | all-to-all | bytes 524288 | tf_op jit(solution)/shard_map/all_to_all | solution.py:151
  84.3 0.8 reshape.235
  (63 shorter events, 6.6 us)
Async XLA Ops:
  0.0 1.2 %copy-start = (bf16[1,1,2,256,256]{4,3,2,1,0:T(8,128)(2,1)S(1)}, bf16[1,1,2,256,256]{4,3,2,1,0:T(8,128)(2,1)}, u32[]{:S(2)}) copy-start(bf16[1,1,2,256,256]{4,3,2,1,0:T(8,128)(2,1)} %param.7) | copy-start | bytes 786436
  0.0 1.2 %copy-start.1 = (bf16[1,2,256,256]{3,2,1,0:T(8,128)(2,1)S(1)}, bf16[1,2,256,256]{3,2,1,0:T(8,128)(2,1)}, u32[]{:S(2)}) copy-start(bf16[1,2,256,256]{3,2,1,0:T(8,128)(2,1)} %param.8) | copy-start | bytes 786436
  2.7 4.4 %copy-start.2 = (bf16[1,1,2,256,256]{4,3,2,1,0:T(8,128)(2,1)S(1)}, bf16[1,1,2,256,256]{4,3,2,1,0:T(8,128)(2,1)}, u32[]{:S(2)}) copy-start(bf16[1,1,2,256,256]{4,3,2,1,0:T(8,128)(2,1)} %param.6) | copy-start | bytes 786436
  2.7 13.1 %all-to-all-start.1 = ((bf16[2,1,2,256,256]{4,3,2,1,0:T(8,128)(2,1)}), bf16[2,1,2,256,256]{4,3,2,1,0:T(8,128)(2,1)S(1)}, u32[]{:S(2)}, u32[]{:S(2)}) async-start(bf16[2,1,2,256,256]{4,3,2,1,0:T(8,128)(2,1)} %fusion.40), calls=%async_computation.1 | async-start | bytes 1048576 | tf_op jit(solution)/shard_map/all_to_all | solution.py:110
  15.8 16.9 %all-to-all-start = ((f32[2,1,2,256,256]{4,3,2,1,0:T(8,128)}), f32[2,1,2,256,256]{4,3,2,1,0:T(8,128)S(1)}, u32[]{:S(2)}, u32[]{:S(2)}) async-start(f32[2,1,2,256,256]{4,3,2,1,0:T(8,128)} %fusion.33), calls=%async_computation | async-start | bytes 2097152 | tf_op jit(solution)/shard_map/all_to_all | solution.py:113
  67.6 1.0 %copy-start.3 = (bf16[1,32,4096]{2,1,0:T(8,128)(2,1)S(1)}, bf16[1,32,4096]{2,1,0:T(8,128)(2,1)}, u32[]{:S(2)}) copy-start(bf16[1,32,4096]{2,1,0:T(8,128)(2,1)} %param.9) | copy-start | bytes 786436
